TPU v7x, 32 devices: a whole 2x2x4 slice. The times are simulated.
32 devices in a mesh: dp: 4 (over z), tensor: 8 (over y, x, core).
Axes of the slice: x: 2, y: 2, z: 4, core: 2. Of those that a mesh axis runs over, the one named last changes fastest.
Arguments:
- activations: bfloat16 [1024, 27648], P('dp', 'tensor'), may hold values from -6 to 6
- left_factor: float32 [216, 216], replicated, may hold values from -2 to 3, as said below
- right_factor: float32 [128, 128], replicated, may hold values from -2 to 3, as said below
- clip_scale: float32 [128, 216], replicated, may hold values from 0.5 to 3
- weight_rows: bfloat16 [27648, 5120], P('tensor'), may hold values from -0.0390625 to 0.0390625
- target: bfloat16 [1024, 5120], P('dp'), may hold values from -6 to 6
Outputs:
- grad_left: float32 [216, 216], replicated
- grad_right: float32 [128, 128], replicated
- grad_input: float32 [1024, 27648], P('dp', 'tensor')
Inputs may be any that keep to these rules, and one draw needn't show every extreme that they name: `left_factor`: the identity plus independent entries of order one over the square root of 216. `right_factor`: the identity plus independent entries of order one over the square root of 128.
All inputs are finite; a program needn't handle non-finite values.
Results may differ from a plain program's by a relative error of at most 0.007.
Values may be sent and summed in bfloat16 or wider, within the bound.
A program may use at most 128 MiB of HBM per device.

v0:
```python
import jax
import jax.numpy as jnp
from jax import lax
from jax.sharding import PartitionSpec as P


def local(activations, left_factor, right_factor, clip_scale, weight_rows, target):
    highest = lax.Precision.HIGHEST
    tok_rows = activations.shape[0]
    width_left = left_factor.shape[0]
    local_right = activations.shape[1] // width_left
    inputs = activations.reshape(tok_rows, local_right, width_left)
    moved = lax.all_to_all(inputs, "tensor", split_axis=0, concat_axis=1, tiled=True)
    mixed = jnp.einsum("tji,ik->tjk", moved.astype(jnp.float32), left_factor, precision=highest)
    rotated = jnp.einsum("jl,tjk->tlk", right_factor, mixed, precision=highest)
    bounded = jnp.tanh(rotated / clip_scale)
    clipped = (clip_scale * bounded).astype(jnp.bfloat16)
    clipped_back = lax.all_to_all(clipped, "tensor", split_axis=1, concat_axis=0, tiled=True)
    partial_out = jnp.dot(
        clipped_back.reshape(tok_rows, -1), weight_rows, preferred_element_type=jnp.float32
    )
    total = lax.psum(partial_out, "tensor")
    out_grad = (total - target.astype(jnp.float32)).astype(jnp.bfloat16)
    clipped_grad = lax.dot_general(
        out_grad, weight_rows, (((1,), (1,)), ((), ())), preferred_element_type=jnp.float32
    )
    clipped_grad = clipped_grad.reshape(tok_rows, local_right, width_left)
    grad_owned = lax.all_to_all(clipped_grad, "tensor", split_axis=0, concat_axis=1, tiled=True)
    rotated_grad = grad_owned * (1.0 - bounded * bounded)
    mixed_grad = jnp.einsum("jl,tlk->tjk", right_factor, rotated_grad, precision=highest)
    right_part = jnp.einsum("tjk,tlk->jl", mixed, rotated_grad, precision=highest)
    grad_back = lax.all_to_all(mixed_grad, "tensor", split_axis=1, concat_axis=0, tiled=True)
    input_grad = jnp.einsum("tjk,ik->tji", grad_back, left_factor, precision=highest).reshape(
        tok_rows, -1
    )
    left_part = jnp.einsum("tji,tjk->ik", inputs.astype(jnp.float32), grad_back, precision=highest)
    left_sum, right_sum = lax.psum((left_part, right_part), ("dp", "tensor"))
    return (left_sum, right_sum, input_grad)


def solution(mesh):
    placed = (P("dp", "tensor"), P(), P(), P(), P("tensor", None), P("dp", None))
    return jax.shard_map(
        local, mesh=mesh, in_specs=placed, out_specs=(P(), P(), P("dp", "tensor")), check_vma=False
    )
```

profile of v0, /device:TPU:8, one launch (start us, length us, event | category | flops | bytes accessed | tf_op | source)
XLA Modules:
  0.0 508.3 jit_solution(451690624203319944)
XLA Ops:
  9.9 3.0 copy.32
  12.9 30.3 %all_to_all.69 = bf16[256,16,216]{2,1,0:T(8,128)(2,1)S(1)} all-to-all(bf16[256,16,216]{2,1,0:T(8,128)(2,1)} %copy.32), channel_id=1, replica_groups=mesh['dp'=4,'tensor'=8] {'tensor'}, dimensions={0} | all-to-all | bytes 3538944 | tf_op jit(solution)/shard_map/all_to_all | solution.py:13
  45.7 4.7 multiply_convert_fusion
  50.4 4.5 copy.36
  54.9 30.1 %all_to_all.70 = bf16[32,128,216]{2,0,1:T(8,128)(2,1)S(1)} all-to-all(bf16[32,128,216]{2,0,1:T(8,128)(2,1)} %copy.36), channel_id=1, replica_groups=mesh['dp'=4,'tensor'=8] {'tensor'}, dimensions={1} | all-to-all | bytes 3538944 | tf_op jit(solution)/shard_map/all_to_all | solution.py:18
  87.6 5.2 %reshape.21 = bf16[256,3456]{1,0:T(8,128)(2,1)} reshape(bf16[8,32,16,216]{3,2,1,0:T(8,128)(2,1)} %copy.38) | data formatting | bytes 3538944 | tf_op jit(solution)/shard_map/reshape | solution.py:20
  92.8 18.0 %fusion.12 = f32[256,5120]{1,0:T(8,128)} fusion(bf16[256,3456]{1,0:T(8,128)(2,1)} %reshape.21, bf16[3456,5120]{1,0:T(8,128)(2,1)} %param.10), kind=kOutput, calls=%fused_computation.18 | convolution fusion | flops 9059696640 | bytes 42401792 | tf_op jit(solution)/shard_map/dot_general | solution.py:19
  110.8 91.8 %all-reduce.4.cloned.1.call-done = f32[256,5120]{1,0:T(8,128)} async-done(((f32[256,5120]{1,0:T(8,128)}), f32[256,5120]{1,0:T(8,128)}) %all-reduce.4.cloned.1.call-update) | async-done | bytes 5242896 | tf_op jit(solution)/shard_map/psum | solution.py:22
  202.6 19.4 %fusion.1 = f32[256,3456]{0,1:T(8,128)} fusion(bf16[3456,5120]{1,0:T(8,128)(2,1)} %param.10, f32[256,5120]{1,0:T(8,128)} %all-reduce.4.cloned.1.call-done, bf16[256,5120]{1,0:T(8,128)(2,1)} %param.11), kind=kOutput, calls=%fused_computation.5 | convolution fusion | flops 9063628800 | bytes 46792704 | tf_op jit(solution)/shard_map/dot_general | solution.py:24
  222.0 5.3 %copy.40 = f32[256,16,216]{2,1,0:T(8,128)} copy(f32[256,16,216]{0,2,1:T(8,128)} %bitcast.63) | data formatting | bytes 7077888 | tf_op jit(solution)/shard_map/reshape | solution.py:27
  227.3 52.6 %all_to_all.71 = f32[256,16,216]{2,1,0:T(8,128)S(1)} all-to-all(f32[256,16,216]{2,1,0:T(8,128)} %copy.40), channel_id=1, replica_groups=mesh['dp'=4,'tensor'=8] {'tensor'}, dimensions={0} | all-to-all | bytes 7077888 | tf_op jit(solution)/shard_map/all_to_all | solution.py:28
  279.9 2.7 copy.41
  282.6 5.5 %copy.42 = f32[32,128,216]{1,2,0:T(8,128)} copy(f32[32,128,216]{2,1,0:T(8,128)} %bitcast.55) | data formatting | bytes 7077888 | tf_op jit(solution)/shard_map/all_to_all | solution.py:28
  288.1 6.4 %convolution_bitcast_fusion = f32[32,128,216]{1,2,0:T(8,128)} fusion(f32[32,128,216]{1,2,0:T(8,128)} %copy.42, f32[32,128,216]{1,2,0:T(8,128)} %get-tuple-element.15, f32[128,128]{1,0:T(8,128)S(1)} %copy-done.2), kind=kOutput, calls=%fused_computation.6 | convolution fusion | flops 1361608704 | bytes 10682368 | tf_op jit(solution)/shard_map/jl,tlk->tjk/dot_general | solution.py:30
  294.5 5.3 %copy.43 = f32[32,128,216]{2,0,1:T(8,128)} copy(f32[32,128,216]{1,2,0:T(8,128)} %convolution_bitcast_fusion) | data formatting | bytes 7077888 | tf_op jit(solution)/shard_map/jl,tlk->tjk/transpose | solution.py:30
  299.7 4.6 all-to-all-start.3
  304.5 10.7 %fusion.3 = f32[128,128]{1,0:T(8,128)} fusion(f32[32,128,216]{1,2,0:T(8,128)} %copy-done.1, f32[32,128,216]{1,2,0:T(8,128)} %copy.42, f32[32,128,216]{1,2,0:T(8,128)} %get-tuple-element.15), kind=kOutput, calls=%fused_computation.9 | convolution fusion | flops 1361608704 | bytes 10682368 | tf_op jit(solution)/shard_map/tjk,tlk->jl/dot_general | solution.py:31
  315.3 38.1 %all-to-all-done.3 = f32[32,128,216]{2,0,1:T(8,128)} async-done(((f32[32,128,216]{2,0,1:T(8,128)}), f32[32,128,216]{2,0,1:T(8,128)}, u32[]{:S(2)}, u32[]{:S(2)}) %all-to-all-start.3) | async-done | bytes 3538976 | tf_op jit(solution)/shard_map/all_to_all | solution.py:32
  353.4 6.5 %copy.45 = f32[8,32,16,216]{3,2,1,0:T(8,128)} copy(f32[8,32,16,216]{3,1,2,0:T(8,128)} %bitcast.17) | data formatting | bytes 7077888 | tf_op jit(solution)/shard_map/all_to_all | solution.py:32
  359.9 5.1 %copy.46 = f32[256,16,216]{0,2,1:T(8,128)} copy(f32[256,16,216]{2,1,0:T(8,128)} %bitcast.56) | data formatting | bytes 7077888 | tf_op jit(solution)/shard_map/all_to_all | solution.py:32
  365.0 4.6 convolution_bitcast_fusion.1
  369.6 7.1 %fusion.4 = f32[256,16,216]{0,2,1:T(8,128)} fusion(f32[256,16,216]{0,2,1:T(8,128)} %copy.46, f32[216,216]{1,0:T(8,128)S(1)} %copy-done), kind=kOutput, calls=%fused_computation.10 | convolution fusion | flops 2293235712 | bytes 7264512 | tf_op jit(solution)/shard_map/tjk,ik->tji/dot_general | solution.py:33
  376.7 5.2 %copy.49 = f32[256,3456]{1,0:T(8,128)} copy(f32[256,3456]{0,1:T(8,128)} %bitcast.59) | data formatting | bytes 7077888
  381.9 116.3 %all-reduce.6.cloned.1.call-done = (f32[216,216]{0,1:T(8,128)}, f32[128,128]{1,0:T(8,128)}) async-done(((f32[216,216]{0,1:T(8,128)}, f32[128,128]{1,0:T(8,128)}), (f32[216,216]{0,1:T(8,128)}, f32[128,128]{1,0:T(8,128)})) %all-reduce.6.cloned.1.call-update) | async-done | bytes 252176 | tf_op jit(solution)/shard_map/psum | solution.py:37
  (18 shorter events, 11.3 us)
Async XLA Ops:
  7.2 36.4 %copy-start = (f32[216,216]{1,0:T(8,128)S(1)}, f32[216,216]{1,0:T(8,128)}, u32[]{:S(2)}) copy-start(f32[216,216]{1,0:T(8,128)} %param.7) | copy-start | bytes 559876
  7.2 195.4 %all-reduce.4.cloned.1.call-start = ((), (), s32[]{:S(2)}) async-start(), calls=%async_computation.4 | async-start | bytes 10485760 | tf_op jit(solution)/shard_map/psum | solution.py:22
  43.5 2.2 copy-start.2
  43.5 2.2 copy-start.3
  45.7 4.7 copy-start.1
  299.7 53.7 %all-to-all-start.3 = ((f32[32,128,216]{2,0,1:T(8,128)}), f32[32,128,216]{2,0,1:T(8,128)}, u32[]{:S(2)}, u32[]{:S(2)}) async-start(f32[32,128,216]{2,0,1:T(8,128)} %copy.43), calls=%async_computation.3 | async-start | bytes 8388608 | tf_op jit(solution)/shard_map/all_to_all | solution.py:32
  304.3 193.9 %all-reduce.6.cloned.1.call-start = ((), (), s32[]{:S(2)}) async-start(), calls=%async_computation.5 | async-start | bytes 573440 | tf_op jit(solution)/shard_map/psum | solution.py:37
Sparse Core Ops, SparseCore 0:
  110.9 91.6 all-reduce.3
  369.7 128.4 all-reduce.5
where the time goes:
time: 510 us; the launch traced here: 508 us
  waiting for transfers between devices  246 us (48%)
  blocking collectives  113 us (22%)
  matrix products  72.9 us (14%)
  local copies, waits for them, and re-layouts  57 us (11%)
  between operations  14.1 us (3%)
    psum x1, waiting for transfers between devices, local(): left_sum, right_sum = lax.psum((left_part, right_part), ('dp', 'tensor'))  116 us
    psum x1, waiting for transfers between devices, local(): total = lax.psum(partial_out, 'tensor')  91.8 us
    all_to_all x1, blocking collectives, local(): lax.all_to_all(clipped_grad, 'tensor', split_axis=0, concat_axis=1, tiled...  52.6 us
    all_to_all x1, waiting for transfers between devices, local(): lax.all_to_all(mixed_grad, 'tensor', split_axis=1, concat_axis=0, tiled=T...  38.1 us
    all_to_all x1, blocking collectives, local(): lax.all_to_all(inputs, 'tensor', split_axis=0, concat_axis=1, tiled=True)  30.3 us
    all_to_all x1, blocking collectives, local(): lax.all_to_all(clipped, 'tensor', split_axis=1, concat_axis=0, tiled=True)  30.1 us
    dot_general x1, matrix products, local(): lax.dot_general(out_grad, weight_rows, (((1,), (1,)), ((), ())), preferre...  19.4 us
    dot_general x1, matrix products, local(): jnp.dot(clipped_back.reshape(tok_rows, -1), weight_rows, preferred_elemen...  18 us
  transfers between devices with their start and end apart: 3, of which 3 were waited for; matrix products, arithmetic and copies ran while one was open for 5% of the time, Pallas kernels for 0%

commit v1 on v0

--- a/solution.py
+++ b/solution.py
@@ -25,7 +25,12 @@
         out_grad, weight_rows, (((1,), (1,)), ((), ())), preferred_element_type=jnp.float32
     )
     clipped_grad = clipped_grad.reshape(tok_rows, local_right, width_left)
-    grad_owned = lax.all_to_all(clipped_grad, "tensor", split_axis=0, concat_axis=1, tiled=True)
+    grad_owned = jnp.concatenate(
+        lax.all_to_all(
+            jnp.stack(jnp.split(clipped_grad, lax.axis_size("tensor"), axis=0)), "tensor", 0, 0
+        ),
+        axis=1,
+    )
     rotated_grad = grad_owned * (1.0 - bounded * bounded)
     mixed_grad = jnp.einsum("jl,tlk->tjk", right_factor, rotated_grad, precision=highest)
     right_part = jnp.einsum("tjk,tlk->jl", mixed, rotated_grad, precision=highest)

time: 510 us -> 540 us (1.059)
  local copies, waits for them, and re-layouts: 57 us -> 81.5 us
    another operation x0 -> x9, local copies, waits for them, and re-layouts: none -> 16.1 us  [local(): jnp.stack(jnp.split(clipped_grad, lax.axis_size('tensor'), axis=0))]
    unnamed x12 -> x23, local copies, waits for them, and re-layouts: 11.1 us -> 21.2 us
    all_to_all x2 -> x0, local copies, waits for them, and re-layouts: 8.18 us -> none  [local(): lax.all_to_all(clipped_grad, 'tensor', split_axis=0, concat_axis=1, tiled...]
  transfers between devices with their start and end apart: 3 -> 3, of which waited for: 3 -> 3; matrix products, arithmetic and copies ran while one was open for 5% -> 4% of each run, Pallas kernels for 0% -> 0%
where the time goes in v1:
time: 540 us; the launch traced here: 534 us
  waiting for transfers between devices  246 us (46%)
  blocking collectives  113 us (21%)
  local copies, waits for them, and re-layouts  81.5 us (15%)
  matrix products  74 us (14%)
  between operations  14.4 us (3%)
    psum x1, waiting for transfers between devices, local(): left_sum, right_sum = lax.psum((left_part, right_part), ('dp', 'tensor'))  116 us
    psum x1, waiting for transfers between devices, local(): total = lax.psum(partial_out, 'tensor')  91.8 us
    all_to_all x1, blocking collectives, local(): lax.all_to_all(jnp.stack(jnp.split(clipped_grad, lax.axis_size('tensor'),...  52.6 us
    all_to_all x1, waiting for transfers between devices, local(): lax.all_to_all(mixed_grad, 'tensor', split_axis=1, concat_axis=0, tiled=T...  38.2 us
    all_to_all x1, blocking collectives, local(): lax.all_to_all(clipped, 'tensor', split_axis=1, concat_axis=0, tiled=True)  30.4 us
    all_to_all x1, blocking collectives, local(): lax.all_to_all(inputs, 'tensor', split_axis=0, concat_axis=1, tiled=True)  30.3 us
    unnamed x23, local copies, waits for them, and re-layouts  21.2 us
    dot_general x1, matrix products, local(): lax.dot_general(out_grad, weight_rows, (((1,), (1,)), ((), ())), preferre...  20.5 us
  transfers between devices with their start and end apart: 3, of which 3 were waited for; matrix products, arithmetic and copies ran while one was open for 4% of the time, Pallas kernels for 0%

profile of v1, /device:TPU:8, one launch (start us, length us, event | category | flops | bytes accessed | tf_op | source)
XLA Modules:
  0.0 534.4 jit_solution(17727284617664468298)
XLA Ops:
  7.2 2.7 copy.44
  9.9 3.0 copy.45
  12.9 30.3 %all_to_all.56 = bf16[256,16,216]{2,1,0:T(8,128)(2,1)S(1)} all-to-all(bf16[256,16,216]{2,1,0:T(8,128)(2,1)} %copy.45), channel_id=1, replica_groups=mesh['dp'=4,'tensor'=8] {'tensor'}, dimensions={0} | all-to-all | bytes 3538944 | tf_op jit(solution)/shard_map/all_to_all | solution.py:13
  45.7 4.7 multiply_convert_fusion
  50.4 4.5 copy.49
  54.9 30.4 %all_to_all.57 = bf16[32,128,216]{2,0,1:T(8,128)(2,1)S(1)} all-to-all(bf16[32,128,216]{2,0,1:T(8,128)(2,1)} %copy.49), channel_id=1, replica_groups=mesh['dp'=4,'tensor'=8] {'tensor'}, dimensions={1} | all-to-all | bytes 3538944 | tf_op jit(solution)/shard_map/all_to_all | solution.py:18
  87.9 5.1 reshape.41
  93.0 17.9 %fusion.13 = f32[256,5120]{1,0:T(8,128)} fusion(bf16[256,3456]{1,0:T(8,128)(2,1)} %reshape.41, bf16[3456,5120]{1,0:T(8,128)(2,1)} %param.10), kind=kOutput, calls=%fused_computation.27 | convolution fusion | flops 9059696640 | bytes 42401792 | tf_op jit(solution)/shard_map/dot_general | solution.py:19
  111.0 91.8 %all-reduce.4.cloned.1.call-done = f32[256,5120]{1,0:T(8,128)} async-done(((f32[256,5120]{1,0:T(8,128)}), f32[256,5120]{1,0:T(8,128)}) %all-reduce.4.cloned.1.call-update) | async-done | bytes 5242896 | tf_op jit(solution)/shard_map/psum | solution.py:22
  202.8 20.5 %fusion.1 = f32[256,3456]{1,0:T(8,128)} fusion(bf16[3456,5120]{1,0:T(8,128)(2,1)} %param.10, f32[256,5120]{1,0:T(8,128)} %all-reduce.4.cloned.1.call-done, bf16[256,5120]{1,0:T(8,128)(2,1)} %param.11), kind=kOutput, calls=%fused_computation.5 | convolution fusion | flops 9063628800 | bytes 46792704 | tf_op jit(solution)/shard_map/dot_general | solution.py:24
  223.3 3.5 fusion.12
  253.2 52.6 %all_to_all.58 = f32[8,32,16,216]{3,2,1,0:T(8,128)S(1)} all-to-all(f32[8,32,16,216]{3,2,1,0:T(8,128)} %constant_dynamic-update-slice_fusion), channel_id=1, replica_groups=mesh['dp'=4,'tensor'=8] {'tensor'}, dimensions={0} | all-to-all | bytes 7077888 | tf_op jit(solution)/shard_map/all_to_all | solution.py:29
  308.4 5.4 %copy.53 = f32[32,128,216]{1,2,0:T(8,128)} copy(f32[32,128,216]{2,1,0:T(8,128)} %bitcast.52) | data formatting | bytes 7077888 | tf_op jit(solution)/shard_map/reshape | solution.py:28
  313.8 6.3 %convolution_bitcast_fusion = f32[32,128,216]{1,2,0:T(8,128)} fusion(f32[32,128,216]{1,2,0:T(8,128)} %copy.53, f32[32,128,216]{1,2,0:T(8,128)} %get-tuple-element.23, f32[128,128]{1,0:T(8,128)S(1)} %copy-done.4), kind=kOutput, calls=%fused_computation.6 | convolution fusion | flops 1361608704 | bytes 10682368 | tf_op jit(solution)/shard_map/jl,tlk->tjk/dot_general | solution.py:35
  320.2 5.2 copy.54
  325.4 4.6 all-to-all-start.3
  330.2 10.7 %fusion.3 = f32[128,128]{1,0:T(8,128)} fusion(f32[32,128,216]{1,2,0:T(8,128)} %copy-done.1, f32[32,128,216]{1,2,0:T(8,128)} %copy.53, f32[32,128,216]{1,2,0:T(8,128)} %get-tuple-element.23), kind=kOutput, calls=%fused_computation.9 | convolution fusion | flops 1361608704 | bytes 10682368 | tf_op jit(solution)/shard_map/tjk,tlk->jl/dot_general | solution.py:36
  340.9 38.2 %all-to-all-done.3 = f32[32,128,216]{2,0,1:T(8,128)} async-done(((f32[32,128,216]{2,0,1:T(8,128)}), f32[32,128,216]{2,0,1:T(8,128)}, u32[]{:S(2)}, u32[]{:S(2)}) %all-to-all-start.3) | async-done | bytes 3538976 | tf_op jit(solution)/shard_map/all_to_all | solution.py:37
  379.1 6.6 %copy.56 = f32[8,32,16,216]{3,2,1,0:T(8,128)} copy(f32[8,32,16,216]{3,1,2,0:T(8,128)} %bitcast.15) | data formatting | bytes 7077888 | tf_op jit(solution)/shard_map/all_to_all | solution.py:37
  385.6 5.3 copy.57
  390.9 4.6 convolution_bitcast_fusion.1
  395.5 7.1 %fusion.4 = f32[256,16,216]{0,2,1:T(8,128)} fusion(f32[256,16,216]{0,2,1:T(8,128)} %copy.57, f32[216,216]{1,0:T(8,128)S(1)} %copy-done), kind=kOutput, calls=%fused_computation.10 | convolution fusion | flops 2293235712 | bytes 7264512 | tf_op jit(solution)/shard_map/tjk,ik->tji/dot_general | solution.py:38
  402.6 5.2 copy.60
  407.8 116.3 %all-reduce.6.cloned.1.call-done = (f32[216,216]{0,1:T(8,128)}, f32[128,128]{1,0:T(8,128)}) async-done(((f32[216,216]{0,1:T(8,128)}, f32[128,128]{1,0:T(8,128)}), (f32[216,216]{0,1:T(8,128)}, f32[128,128]{1,0:T(8,128)})) %all-reduce.6.cloned.1.call-update) | async-done | bytes 252176 | tf_op jit(solution)/shard_map/psum | solution.py:42
  (38 shorter events, 37.4 us)
Async XLA Ops:
  7.2 36.4 %copy-start = (f32[216,216]{1,0:T(8,128)S(1)}, f32[216,216]{1,0:T(8,128)}, u32[]{:S(2)}) copy-start(f32[216,216]{1,0:T(8,128)} %param.7) | copy-start | bytes 559876
  7.2 195.6 %all-reduce.4.cloned.1.call-start = ((), (), s32[]{:S(2)}) async-start(), calls=%async_computation.4 | async-start | bytes 10485760 | tf_op jit(solution)/shard_map/psum | solution.py:22
  43.5 2.2 copy-start.4
  43.5 2.2 copy-start.5
  45.7 4.7 copy-start.1
  229.5 10.4 %copy-start.3 = (f32[32,3456]{1,0:T(8,128)S(1)}, f32[32,3456]{1,0:T(8,128)}, u32[]{:S(2)}) copy-start(f32[32,3456]{1,0:T(8,128)} %get-tuple-element.16) | copy-start | bytes 1327108
  243.0 7.6 %copy-start.2 = (f32[1,32,16,216]{3,2,1,0:T(8,128)S(1)}, f32[1,32,16,216]{3,2,1,0:T(8,128)}, u32[]{:S(2)}) copy-start(f32[1,32,16,216]{3,2,1,0:T(8,128)} %stack.32) | copy-start | bytes 1327108
  325.4 53.7 %all-to-all-start.3 = ((f32[32,128,216]{2,0,1:T(8,128)}), f32[32,128,216]{2,0,1:T(8,128)}, u32[]{:S(2)}, u32[]{:S(2)}) async-start(f32[32,128,216]{2,0,1:T(8,128)} %copy.54), calls=%async_computation.3 | async-start | bytes 8388608 | tf_op jit(solution)/shard_map/all_to_all | solution.py:37
  330.0 194.2 %all-reduce.6.cloned.1.call-start = ((), (), s32[]{:S(2)}) async-start(), calls=%async_computation.5 | async-start | bytes 573440 | tf_op jit(solution)/shard_map/psum | solution.py:42
Sparse Core Ops, SparseCore 0:
  111.1 91.6 all-reduce.3
  395.6 128.4 all-reduce.5
